TPU v7x, 32 devices: a whole 2x2x4 slice. The times are simulated.
32 devices in a mesh: chan: 16 (over z, y, x), tm: 2 (over core).
Axes of the slice: x: 2, y: 2, z: 4, core: 2. Of those that a mesh axis runs over, the one named last changes fastest.
Arguments:
- visibilities: bfloat16 [2, 4, 128, 480], P(None, 'tm', 'chan'), may hold values from -6 to 6
- baseline_coords: float32 [3, 4, 480], P(None, 'tm'), may hold values from -180 to 180
- source_offsets: float32 [2, 20], replicated, may hold values from -0.08 to 0.08
- source_flux: float32 [20, 128], P(None, 'chan'), may hold values from 0.01 to 0.1
- cluster_of_source: int32 [20, 1], replicated, may hold values from 0 to 17
- baseline_stations: int32 [480, 2], replicated, may hold values from 0 to 61, as said below
- station_flags: int32 [62, 4], P(None, 'tm'), may hold values 0 or 1
- local_gains: float32 [2, 2, 128, 18, 62], P(None, 'tm', 'chan'), may hold values from -1.6 to 3.2
- dual_gains: float32 [2, 2, 128, 18, 62], P(None, 'tm', 'chan'), may hold values from -3.5 to 3.5
- penalty: float32 [18], replicated, may hold values from 0.4 to 0.8
Outputs:
- cross_power: float32 [480, 128], P('chan', 'tm')
- dual_update: float32 [2, 2, 128, 18, 62], P(None, 'tm', 'chan')
Inputs may be any that keep to these rules, and one draw needn't show every extreme that they name: `baseline_stations`: row b holds two different stations, the first the smaller; rows repeat a pair only where 480 exceeds the number of station pairs. `cluster_of_source`: every direction has at least one component.
All inputs are finite; a program needn't handle non-finite values. No bound on the sum of `station_flags` on one device may be relied on, other than what follows from the above.
Results may differ from a plain program's by a relative error of at most 0.012.
Values may be sent and summed in bfloat16 or wider, within the bound.
A program may use at most 64 MiB of HBM per device.

v0:
```python
import math

import jax
import jax.numpy as jnp
from jax import lax
from jax.sharding import PartitionSpec as P

HIGHEST = lax.Precision.HIGHEST


def legendre_basis(indices, total):
    coordinate = (2 * indices + 1).astype(jnp.float32) / total - 1.0
    return jnp.stack(
        [jnp.ones_like(coordinate), coordinate, 1.5 * coordinate * coordinate - 0.5], axis=1
    )


def channel_scale(indices, total):
    return 2.0 * math.pi * (0.9 + 0.2 * (indices.astype(jnp.float32) + 0.5) / total)


def blackman_taper(total):
    angles = 2.0 * math.pi / (total - 1) * jnp.arange(total, dtype=jnp.int32).astype(jnp.float32)
    return (
        0.35875
        - 0.48829 * jnp.cos(angles)
        + 0.14128 * jnp.cos(2.0 * angles)
        - 0.01168 * jnp.cos(3.0 * angles)
    )


def delay_table(total):
    indices = jnp.arange(total, dtype=jnp.int32)
    product = indices[:, None] * indices[None, :] % total
    angles = 2.0 * math.pi / total * product.astype(jnp.float32)
    return jnp.concatenate([jnp.cos(angles), jnp.sin(angles)], axis=1).astype(jnp.bfloat16)


def solve_gram(factor, right_side):
    middle = lax.linalg.triangular_solve(factor, right_side, left_side=True, lower=True)
    return lax.linalg.triangular_solve(factor, middle, left_side=True, lower=True, transpose_a=True)


def keep_weight(flags, first, second):
    return ((1.0 - jnp.take(flags, first, axis=0)) * (1.0 - jnp.take(flags, second, axis=0))).T


def source_model(
    coeffs,
    basis,
    first,
    second,
    onehot,
    flux,
    antenna_pair_coordinates,
    offsets,
    depth,
    scale,
    segment_portion,
):
    gain_first = jnp.einsum(
        "fk,krdb->rfdb", basis, jnp.take(coeffs, first, axis=3), precision=HIGHEST
    )
    gain_second = jnp.einsum(
        "fk,krdb->rfdb", basis, jnp.take(coeffs, second, axis=3), precision=HIGHEST
    )
    pair_real = gain_first[0] * gain_second[0] + gain_first[1] * gain_second[1]
    pair_imag = gain_first[1] * gain_second[0] - gain_first[0] * gain_second[1]
    coef_real = jnp.einsum("sd,fdb->sfb", onehot, pair_real, precision=HIGHEST) * flux[:, :, None]
    coef_imag = jnp.einsum("sd,fdb->sfb", onehot, pair_imag, precision=HIGHEST) * flux[:, :, None]
    lag_grid = (
        offsets[0][:, None, None] * antenna_pair_coordinates[0][None]
        + offsets[1][:, None, None] * antenna_pair_coordinates[1][None]
        + depth[:, None, None] * antenna_pair_coordinates[2][None]
    )
    components, frequency_bins, pair_group_extent = coef_real.shape
    sampling_epochs = antenna_pair_coordinates.shape[1]
    iteration_count = components // segment_portion
    pieces = (
        coef_real.reshape(iteration_count, segment_portion, frequency_bins, pair_group_extent),
        coef_imag.reshape(iteration_count, segment_portion, frequency_bins, pair_group_extent),
        lag_grid.reshape(iteration_count, segment_portion, sampling_epochs, pair_group_extent),
    )

    def accumulate(carry, piece):
        part_real, part_imag, part_delay = piece
        angles = scale[None, None, :, None] * part_delay[:, :, None, :]
        cosine = jnp.cos(angles)
        sine_part = jnp.sin(angles)
        real_sum = jnp.sum(part_real[:, None] * cosine + part_imag[:, None] * sine_part, axis=0)
        imag_sum = jnp.sum(part_imag[:, None] * cosine - part_real[:, None] * sine_part, axis=0)
        return ((carry[0] + real_sum, carry[1] + imag_sum), None)

    offset_first_entry = (
        jnp.zeros((sampling_epochs, frequency_bins, pair_group_extent), jnp.float32),
        jnp.zeros((sampling_epochs, frequency_bins, pair_group_extent), jnp.float32),
    )
    (model_real, model_imag), unused = lax.scan(accumulate, offset_first_entry, pieces)
    return (model_real, model_imag)


def shards(
    visibilities,
    baseline_coords,
    source_offsets,
    source_flux,
    cluster_of_source,
    baseline_stations,
    station_flags,
    local_gains,
    dual_gains,
    penalty,
):
    width_chan = source_flux.shape[1]
    groups = lax.axis_size("chan")
    position = lax.axis_index("chan")
    total_chan = width_chan * groups
    directions = penalty.shape[0]
    all_index = jnp.arange(total_chan, dtype=jnp.int32)
    local_index = position * width_chan + jnp.arange(width_chan, dtype=jnp.int32)
    basis_all = legendre_basis(all_index, total_chan)
    basis_local = legendre_basis(local_index, total_chan)
    factor = jnp.linalg.cholesky(jnp.dot(basis_all.T, basis_all, precision=HIGHEST))
    rate = penalty[:, None]
    target = local_gains[:, 0] + dual_gains[:, 0] / rate
    partial_sums = jnp.einsum("fk,rfdp->krdp", basis_local, target, precision=HIGHEST)
    totals = lax.psum(partial_sums, "chan")
    coeffs = solve_gram(factor, totals.reshape(totals.shape[0], -1)).reshape(totals.shape)
    smooth = jnp.einsum("fk,krdp->rfdp", basis_local, coeffs, precision=HIGHEST)
    dual_update = dual_gains + rate * (local_gains - smooth[:, None])
    onehot = (cluster_of_source == jnp.arange(directions, dtype=jnp.int32)[None, :]).astype(
        jnp.float32
    )
    depth = (
        jnp.sqrt(
            1.0 - source_offsets[0] * source_offsets[0] - source_offsets[1] * source_offsets[1]
        )
        - 1.0
    )
    flag_float = station_flags.astype(jnp.float32)
    first = baseline_stations[:, 0]
    second = baseline_stations[:, 1]
    model_real, model_imag = source_model(
        coeffs,
        basis_local,
        first,
        second,
        onehot,
        source_flux,
        baseline_coords,
        source_offsets,
        depth,
        channel_scale(local_index, total_chan),
        4,
    )
    keep = keep_weight(flag_float, first, second)
    residual = (
        keep[None, :, None, :] * (visibilities - jnp.stack([model_real, model_imag]))
    ).astype(jnp.bfloat16)
    regrouped = lax.all_to_all(residual, "chan", split_axis=3, concat_axis=2, tiled=True)
    taper = blackman_taper(total_chan)
    table = delay_table(total_chan)
    norm = 1.0 / jnp.sqrt(jnp.sum(taper * taper))
    tapered = (regrouped * taper[None, None, :, None]).astype(jnp.bfloat16)
    raw = lax.dot_general(
        tapered, table, (((2,), (0,)), ((), ())), preferred_element_type=jnp.float32
    )
    spec_real = (raw[0, :, :, :total_chan] + raw[1, :, :, total_chan:]) * norm
    spec_imag = (raw[1, :, :, :total_chan] - raw[0, :, :, total_chan:]) * norm
    halves = spec_real.shape[0] // 2
    paired_real = spec_real.reshape(halves, 2, spec_real.shape[1], spec_real.shape[2])
    paired_imag = spec_imag.reshape(halves, 2, spec_imag.shape[1], spec_imag.shape[2])
    local_cross = jnp.sum(
        paired_real[:, 0] * paired_real[:, 1] + paired_imag[:, 0] * paired_imag[:, 1], axis=0
    )
    summed = lax.psum_scatter(local_cross, "tm", scatter_dimension=1, tiled=True)
    pair_total = halves * lax.axis_size("tm")
    cross_power = summed / pair_total
    return (cross_power, dual_update)


def solution(mesh):
    in_specs = (
        P(None, "tm", "chan", None),
        P(None, "tm", None),
        P(),
        P(None, "chan"),
        P(),
        P(),
        P(None, "tm"),
        P(None, "tm", "chan", None, None),
        P(None, "tm", "chan", None, None),
        P(),
    )
    out_specs = (P("chan", "tm"), P(None, "tm", "chan", None, None))
    return jax.shard_map(shards, mesh=mesh, in_specs=in_specs, out_specs=out_specs, check_vma=False)
```

profile of v0, /device:TPU:0, one launch (start us, length us, event | category | flops | bytes accessed | tf_op | source)
XLA Modules:
  0.0 146.0 jit_solution(13235573177548644853)
XLA Ops:
  7.2 0.8 fusion.61
  10.2 1.3 fusion.20
  11.8 79.4 %psum.7 = f32[2,18,62,3]{2,3,1,0:T(4,128)S(1)} all-reduce(f32[2,18,62,3]{2,3,1,0:T(4,128)S(1)} %copy.113), channel_id=1, replica_groups=mesh['chan'=16,'tm'=2] {'chan'}, use_global_device_ids=true, to_apply=%region_2.4 | all-reduce | flops 6696 | bytes 53568 | tf_op jit(solution)/shard_map/psum | solution.py:127
  92.5 3.9 %gather_fusion.2 = f32[480,3,2,18]{3,2,1,0:T(2,128)} fusion(f32[3,2,18,62]{2,1,3,0:T(2,128)S(1)} %copy.115, s32[1024]{0:T(1024)S(1)} %pad_clamp_fusion.1), kind=kCustom, calls=%fused_computation.1.clone | custom fusion | bytes 416640 | tf_op jit(solution)/shard_map/jit(_take)/gather | solution.py:62
  96.4 3.8 %gather_fusion.3 = f32[480,3,2,18]{3,2,1,0:T(2,128)S(1)} fusion(f32[3,2,18,62]{2,1,3,0:T(2,128)S(1)} %copy.115, s32[1024]{0:T(1024)S(1)} %pad_clamp_fusion), kind=kCustom, calls=%fused_computation.3.clone | custom fusion | bytes 416640 | tf_op jit(solution)/shard_map/jit(_take)/gather | solution.py:65
  100.4 1.6 %gather_fusion = f32[480,2]{1,0:T(8,128)} fusion(f32[62,2]{1,0:T(8,128)S(1)} %convert_element_type.73, s32[1024]{0:T(1024)S(1)} %pad_clamp_fusion.1), kind=kCustom, calls=%fused_computation.clone | custom fusion | bytes 9600 | tf_op jit(solution)/shard_map/jit(_take)/gather | solution.py:45
  102.0 1.6 %gather_fusion.1 = f32[480,2]{1,0:T(8,128)} fusion(f32[62,2]{1,0:T(8,128)S(1)} %convert_element_type.73, s32[1024]{0:T(1024)S(1)} %pad_clamp_fusion), kind=kCustom, calls=%fused_computation.2.clone | custom fusion | bytes 9600 | tf_op jit(solution)/shard_map/jit(_take)/gather | solution.py:45
  103.7 2.7 %select_bitcast_fusion.1 = f32[3,2,18,480]{2,1,0,3:T(2,128)S(1)} fusion(f32[480,3,2,18]{3,2,1,0:T(2,128)} %gather_fusion.2, pred[480]{0:T(512)(128)(4,1)S(1)} %get-tuple-element.124), kind=kLoop, calls=%fused_computation.22 | loop fusion | flops 51840 | bytes 415200 | tf_op jit(solution)/shard_map/jit(_take)/select_n | solution.py:62
  106.4 1.7 %copy.116 = f32[3,2,18,480]{3,0,2,1:T(4,128)S(1)} copy(f32[3,2,18,480]{2,1,0,3:T(2,128)S(1)} %select_bitcast_fusion.1) | data formatting | bytes 414720 | tf_op jit(solution)/shard_map/jit(_take)/select_n | solution.py:62
  108.1 0.7 convolution_bitcast_fusion.1
  108.8 1.6 %select_bitcast_fusion = f32[3,2,18,480]{2,1,0,3:T(2,128)S(1)} fusion(f32[480,3,2,18]{3,2,1,0:T(2,128)S(1)} %gather_fusion.3, pred[480]{0:T(512)(128)(4,1)S(1)} %get-tuple-element.123), kind=kLoop, calls=%fused_computation.21 | loop fusion | flops 51840 | bytes 415200 | tf_op jit(solution)/shard_map/jit(_take)/select_n | solution.py:65
  110.5 1.7 %copy.118 = f32[3,2,18,480]{3,0,2,1:T(4,128)S(1)} copy(f32[3,2,18,480]{2,1,0,3:T(2,128)S(1)} %select_bitcast_fusion) | data formatting | bytes 414720 | tf_op jit(solution)/shard_map/jit(_take)/select_n | solution.py:65
  112.2 0.7 convolution_bitcast_fusion
  114.9 3.4 %while.13 = (s32[]{:T(128)}, f32[2,8,480]{2,1,0:T(8,128)S(1)}, f32[2,8,480]{2,1,0:T(8,128)S(1)}, f32[5,4,8,480]{3,2,1,0:T(8,128)S(1)}, f32[5,4,2,480]{3,2,1,0:T(...) while((s32[]{:T(128)}, f32[2,8,480]{2,1,0:T(8,128)S(1)}, ...), condition=%wide.region_6.9_spmd.clone, body=%wide.region_3.0_spmd.clone.sunk | while | flops 291891 | bytes 660660 | solution.py:98
  118.7 0.7 copy.123
  119.4 1.1 reshape.251
  120.4 3.5 %all-to-all-start = ((bf16[16,2,480]{2,1,0:T(2,128)(2,1)}), bf16[16,2,480]{2,1,0:T(2,128)(2,1)S(1)}, u32[]{:S(2)}, u32[]{:S(2)}) async-start(bf16[16,2,480]{2,1,0:T(2,128)(2,1)} %reshape.251), calls=%async_computation | async-start | bytes 65536 | tf_op jit(solution)/shard_map/all_to_all | solution.py:160
  124.3 0.7 multiply_reduce_fusion
  125.7 5.6 %all-to-all-done = bf16[16,2,480]{2,1,0:T(2,128)(2,1)S(1)} async-done(((bf16[16,2,480]{2,1,0:T(2,128)(2,1)}), bf16[16,2,480]{2,1,0:T(2,128)(2,1)S(1)}, u32[]{:S(2)}, u32[]{:S(2)}) %all-to-all-start) | async-done | bytes 30752 | tf_op jit(solution)/shard_map/all_to_all | solution.py:160
  131.6 0.9 copy.124
  132.8 0.7 copy.137
  133.6 1.1 fusion.13
  134.7 3.1 %reduce-scatter.4.cloned.1.call-done = f32[64,30]{1,0:T(8,128)} async-done(((f32[128,30]{1,0:T(8,128)}), f32[64,30]{1,0:T(8,128)}) %reduce-scatter.4.cloned.1.call-update) | async-done | bytes 7696
  137.7 0.8 copy.138
  (114 shorter events, 10.7 us)
Async XLA Ops:
  8.0 95.7 %copy-start.11 = (pred[480]{0:T(512)(128)(4,1)}, pred[480]{0:T(512)(128)(4,1)S(1)}, u32[]{:S(2)}) copy-start(pred[480]{0:T(512)(128)(4,1)S(1)} %get-tuple-element.124) | copy-start | bytes 1444
  10.2 90.1 %copy-start.14 = (s32[62,2]{0,1:T(2,128)S(1)}, s32[62,2]{0,1:T(2,128)}, u32[]{:S(2)}) copy-start(s32[62,2]{0,1:T(2,128)} %param.22) | copy-start | bytes 1492
  91.9 0.6 copy-start.4
  112.1 0.9 copy-start.9
  112.2 0.9 copy-start.13
  113.1 1.4 copy-start.15
  113.1 1.6 %copy-start.10 = (f32[3,2,480]{2,1,0:T(2,128)S(1)}, f32[3,2,480]{2,1,0:T(2,128)}, u32[]{:S(2)}) copy-start(f32[3,2,480]{2,1,0:T(2,128)} %param.17) | copy-start | bytes 34564
  113.1 1.8 %copy-start = (f32[2,8,480]{2,1,0:T(8,128)S(1)}, f32[2,8,480]{2,1,0:T(8,128)}, u32[]{:S(2)}) copy-start(f32[2,8,480]{2,1,0:T(8,128)} %custom-call.10) | copy-start | bytes 92164
  113.1 1.8 %copy-start.1 = (f32[2,8,480]{2,1,0:T(8,128)S(1)}, f32[2,8,480]{2,1,0:T(8,128)}, u32[]{:S(2)}) copy-start(f32[2,8,480]{2,1,0:T(8,128)} %custom-call.9) | copy-start | bytes 92164
  114.9 3.4 %copy-start.2 = (f32[480,2]{1,0:T(8,128)S(1)}, f32[480,2]{1,0:T(8,128)}, u32[]{:S(2)}) copy-start(f32[480,2]{1,0:T(8,128)} %gather_fusion) | copy-start | bytes 11524
  114.9 3.4 %copy-start.3 = (f32[480,2]{1,0:T(8,128)S(1)}, f32[480,2]{1,0:T(8,128)}, u32[]{:S(2)}) copy-start(f32[480,2]{1,0:T(8,128)} %gather_fusion.1) | copy-start | bytes 11524
  114.9 3.4 %copy-start.12 = (pred[480]{0:T(512)(128)(4,1)S(1)}, pred[480]{0:T(512)(128)(4,1)}, u32[]{:S(2)}) copy-start(pred[480]{0:T(512)(128)(4,1)} %copy-done.11) | copy-start | bytes 1444
  114.9 3.7 %copy-start.8 = (bf16[2,2,8,480]{3,2,1,0:T(8,128)(2,1)S(1)}, bf16[2,2,8,480]{3,2,1,0:T(8,128)(2,1)}, u32[]{:S(2)}) copy-start(bf16[2,2,8,480]{3,2,1,0:T(8,128)(2,1)} %param.16) | copy-start | bytes 92164
  119.3 14.2 %copy-start.5 = (f32[3,2,18,62]{3,0,2,1:T(4,128)S(1)}, f32[3,2,18,62]{3,0,2,1:T(4,128)}, u32[]{:S(2)}) copy-start(f32[3,2,18,62]{3,0,2,1:T(4,128)} %copy-done.4) | copy-start | bytes 80356
  119.3 14.2 %copy-start.6 = (f32[2,1,8,18,62]{4,2,3,1,0:T(8,128)S(1)}, f32[2,1,8,18,62]{4,2,3,1,0:T(8,128)}, u32[]{:S(2)}) copy-start(f32[2,1,8,18,62]{4,2,3,1,0:T(8,128)} %param.24) | copy-start | bytes 214276
  119.4 14.2 %copy-start.7 = (f32[2,1,8,18,62]{4,2,3,1,0:T(8,128)S(1)}, f32[2,1,8,18,62]{4,2,3,1,0:T(8,128)}, u32[]{:S(2)}) copy-start(f32[2,1,8,18,62]{4,2,3,1,0:T(8,128)} %param.23) | copy-start | bytes 214276
  119.4 14.2 %copy-start.16 = (f32[18]{0:T(128)S(1)}, f32[18]{0:T(128)}, u32[]{:S(2)}) copy-start(f32[18]{0:T(128)} %param.25) | copy-start | bytes 220
  120.4 10.9 %all-to-all-start = ((bf16[16,2,480]{2,1,0:T(2,128)(2,1)}), bf16[16,2,480]{2,1,0:T(2,128)(2,1)S(1)}, u32[]{:S(2)}, u32[]{:S(2)}) async-start(bf16[16,2,480]{2,1,0:T(2,128)(2,1)} %reshape.251), calls=%async_computation | async-start | bytes 65536 | tf_op jit(solution)/shard_map/all_to_all | solution.py:160
  123.9 13.8 %reduce-scatter.4.cloned.1.call-start = ((), (), s32[]{:S(2)}) async-start(), calls=%async_computation.2 | async-start | bytes 98304
Sparse Core Ops, SparseCore 0:
  133.7 3.9 reduce-scatter.3
where the time goes:
time: 146 us
  blocking collectives  79.4 us (54%)
  local copies, waits for them, and re-layouts  21.6 us (15%)
  between operations  15.3 us (10%)
  other arithmetic  11.4 us (8%)
  waiting for transfers between devices  8.69 us (6%)
  matrix products  5.88 us (4%)
  starting transfers between devices  3.53 us (2%)
    psum x1, blocking collectives, shards(): totals = lax.psum(partial_sums, 'chan')  79.4 us
    all_to_all x1, waiting for transfers between devices, shards(): lax.all_to_all(residual, 'chan', split_axis=3, concat_axis=2, tiled=True)  5.62 us
    gather x1, local copies, waits for them, and re-layouts, source_model(): jnp.take(coeffs, first, axis=3)  3.91 us
    gather x1, local copies, waits for them, and re-layouts, source_model(): jnp.take(coeffs, second, axis=3)  3.85 us
    unnamed x39, local copies, waits for them, and re-layouts  3.55 us
    all_to_all x1, starting transfers between devices, shards(): lax.all_to_all(residual, 'chan', split_axis=3, concat_axis=2, tiled=True)  3.48 us
    unnamed x2, waiting for transfers between devices  3.07 us
  transfers between devices with their start and end apart: 2, of which 2 were waited for; matrix products, arithmetic and copies ran while one was open for 1% of the time, Pallas kernels for 0%

commit v1 on v0

v1 whole, which is shorter than its diff:
```python
import math

import jax
import jax.numpy as jnp
import numpy as np
from jax import lax
from jax.experimental import pallas as pl
from jax.experimental.pallas import tpu as pltpu
from jax.sharding import PartitionSpec as P

HIGHEST = lax.Precision.HIGHEST
MESH = pl.DeviceIdType.MESH
TERMS = 3
F32 = jnp.float32
BF16 = jnp.bfloat16


def turn_polynomials():
    nodes = np.cos(np.pi * (np.arange(400) + 0.5) / 400) * 0.125 + 0.125
    root = np.sqrt(nodes)
    cosine = np.polynomial.Chebyshev.fit(nodes, np.cos(2 * np.pi * root), 6)
    sine = np.polynomial.Chebyshev.fit(nodes, np.sin(2 * np.pi * root) / root, 6)
    pick = lambda fit: [float(c) for c in fit.convert(kind=np.polynomial.Polynomial).coef]
    return pick(cosine), pick(sine)


COS_TERMS, SIN_TERMS = turn_polynomials()


def horner(terms, z):
    value = jnp.full_like(z, terms[-1])
    for term in terms[-2::-1]:
        value = value * z + term
    return value


def taper_values(total):
    angles = 2.0 * np.pi / (total - 1) * np.arange(total)
    return 0.35875 - 0.48829 * np.cos(angles) + 0.14128 * np.cos(2 * angles) - 0.01168 * np.cos(3 * angles)


def delay_tables(total, parts):
    index = np.arange(total)
    angles = 2.0 * np.pi / total * (index[:, None] * index[None, :] % total)
    wide = total // parts
    cosine = np.cos(angles).reshape(total, parts, wide)
    sine = np.sin(angles).reshape(total, parts, wide)
    return jnp.asarray(np.concatenate([cosine, sine], axis=2).transpose(1, 0, 2), BF16)


def gram_inverse(total):
    x = (2.0 * np.arange(total) + 1.0) / total - 1.0
    basis = np.stack([np.ones_like(x), x, 1.5 * x * x - 0.5], axis=1)
    return np.linalg.inv(basis.T @ basis)


def ceil_to(value, step):
    return -(-value // step) * step


def split_groups(groups):
    low = 1
    while low * 2 * low * 2 <= groups and groups % (low * 2) == 0:
        low *= 2
    return low, groups // low


def iota(shape, dim):
    return lax.broadcasted_iota(jnp.int32, shape, dim)


def make_kernel(cfg):
    groups, parts, width, dirs, stations = (cfg[k] for k in ("groups", "parts", "width", "dirs", "stations"))
    sources, epochs, base, own, pad = (cfg[k] for k in ("sources", "epochs", "base", "own", "pad"))
    low, high, rows, total = (cfg[k] for k in ("low", "high", "rows", "total"))
    count = groups * parts
    lanes = groups * pad
    half = cfg["half"]
    inverse = gram_inverse(total)
    norm2 = 1.0 / float(np.sum(taper_values(total) ** 2))
    pair_total = (epochs // 2) * parts
    slab = 2 * epochs * pad
    per_tile = 128 // pad

    def kernel(
        cluster, vis, coords, offsets, flux, pairs, flags, local, dual, penalty, taper, table,
        cross_out, dual_out,
        packed, sum_send, sum_recv, part_send, part_recv, perm, onehot, delay, wave_c, wave_s,
        pair_r, pair_i, out_send, out_recv,
        s1_send, s1_recv, s2_send, s2_recv, a_send, a_recv,
    ):
        chan = lax.axis_index("chan")
        part = lax.axis_index("tm")
        me = part * groups + chan
        barrier = pltpu.get_barrier_semaphore()

        def others(act):
            for dm in range(parts):
                m = lax.rem(part + dm, parts)

                def step(i, carry, m=m):
                    act(lax.rem(chan + i, groups), m)
                    return carry

                first = 1 if dm == 0 else 0
                lax.fori_loop(first, groups, step, 0, unroll=groups <= 16)

        others(lambda c, m: pl.semaphore_signal(barrier, inc=1, device_id={"chan": c, "tm": m}, device_id_type=MESH))

        tall = dirs * width
        rate = jnp.sum(
            jnp.where(iota((tall, dirs), 0) // width == iota((tall, dirs), 1), penalty[...], 0.0), axis=1, keepdims=True
        )
        packed[...] = jnp.zeros_like(packed)
        inverse_rate = 1.0 / rate
        for r in range(2):
            packed[:, r * half : r * half + stations] = local[r] + dual[r] * inverse_rate

        def coordinate(f):
            return (2 * (chan * width + f) + 1).astype(F32) / total - 1.0

        def term_of(row):
            k = sum((row >= dirs * i).astype(jnp.int32) for i in range(1, TERMS + 1))
            return k, row - k * dirs

        row, col = iota((rows, tall), 0), iota((rows, tall), 1)
        k, d = term_of(row)
        x = coordinate(lax.rem(col, width))
        value = jnp.where(k == 0, 1.0, jnp.where(k == 1, x, 1.5 * x * x - 0.5))
        weights = jnp.where((d == col // width) & (k < TERMS), value, 0.0)
        sum_send[...] = jnp.dot(weights, packed[...], precision=HIGHEST, preferred_element_type=F32)

        lo, hi = lax.rem(chan, low), chan // low
        pl.semaphore_wait(barrier, count - 1)

        def stage(src, dst, send, recv, size, mine, address):
            copies = []
            for i in range(1, size):
                copies.append(
                    pltpu.make_async_remote_copy(
                        src_ref=src,
                        dst_ref=dst.at[i - 1],
                        send_sem=send.at[i - 1],
                        recv_sem=recv.at[i - 1],
                        device_id={"chan": address(lax.rem(mine + i, size)), "tm": part},
                        device_id_type=MESH,
                    )
                )
            for copy in copies:
                copy.start()
            return copies

        first = stage(sum_send, sum_recv, s1_send, s1_recv, low, lo, lambda t: hi * low + t)

        prow, pcol = iota((base, lanes), 0), iota((base, lanes), 1)
        inner = lax.rem(pcol, pad)
        perm[...] = jnp.where((prow == (pcol // pad) * own + inner) & (inner < own), 1.0, 0.0).astype(BF16)
        place = perm[...]
        station_rows = jnp.dot(pairs[...].astype(F32).astype(BF16), place, preferred_element_type=F32).astype(jnp.int32)
        srow = iota((2 * half, lanes), 0)
        for side in range(2):
            line = station_rows[side : side + 1, :]
            for r in range(2):
                onehot[r, :, side * lanes : (side + 1) * lanes] = jnp.where(srow == line + r * half, 1.0, 0.0).astype(BF16)

        def placed(value):
            out = None
            for _ in range(3):
                piece = value.astype(BF16)
                value = value - piece.astype(F32)
                moved = jnp.dot(piece, place, preferred_element_type=F32)
                out = moved if out is None else out + moved
            return out

        u, v, w = (placed(coords[i]) for i in range(3))
        same = iota((sources, sources), 0) == iota((sources, sources), 1)
        column = lambda line: jnp.sum(jnp.where(same, line, 0.0), axis=1, keepdims=True)
        l, m = offsets[0:1, :], offsets[1:2, :]
        lc, mc, nc = column(l), column(m), column(jnp.sqrt(1.0 - l * l - m * m) - 1.0)
        for t in range(epochs):
            delay[t] = lc * u[t : t + 1] + mc * v[t : t + 1] + nc * w[t : t + 1]
        vis_placed = [
            [jnp.dot(vis[r, t].astype(F32).astype(BF16), place, preferred_element_type=F32) for t in range(epochs)]
            for r in range(2)
        ]
        unflagged = (1.0 - flags[...].astype(F32)).astype(BF16)
        kept = jnp.dot(unflagged, onehot[0, 0:stations, :], preferred_element_type=F32)
        keep = kept[:, :lanes] * kept[:, lanes:]
        channel = (chan * width + iota((width, 1), 0)).astype(F32)
        rate_turns = 0.9 + 0.2 * (channel + 0.5) / total

        def phases(begin, end):
            for s in range(begin, end):
                scale = flux[:, s : s + 1]
                for t in range(epochs):
                    turns = rate_turns * delay[t, s : s + 1, :]
                    turns = turns - jnp.round(turns)
                    z = turns * turns
                    wave_c[s, t] = scale * horner(COS_TERMS, z)
                    wave_s[s, t] = scale * (turns * horner(SIN_TERMS, z))

        phases(0, sources // 2)
        acc = sum_send[...]
        for i, copy in enumerate(first):
            copy.wait_recv()
            acc = acc + sum_recv[i]
        part_send[...] = acc
        second = stage(part_send, part_recv, s2_send, s2_recv, high, hi, lambda t: t * low + lo)
        phases(sources // 2, sources)
        vrow, vcol = iota((tall, rows), 0), iota((tall, rows), 1)
        k, d = term_of(vcol)
        x = coordinate(lax.rem(vrow, width))
        x2 = 1.5 * x * x - 0.5
        value = jnp.zeros_like(x)
        for i in range(TERMS):
            mixed = float(inverse[0, i]) + x * float(inverse[1, i]) + x2 * float(inverse[2, i])
            value = jnp.where(k == i, mixed, value)
        spread = jnp.where((d == vrow // width) & (k < TERMS), value, 0.0)
        for i, copy in enumerate(second):
            copy.wait_recv()
            acc = acc + part_recv[i]

        smooth = jnp.dot(spread, acc, precision=HIGHEST, preferred_element_type=F32)
        big = smooth.astype(BF16)
        small = (smooth - big.astype(F32)).astype(BF16)
        gains = [
            jnp.dot(big, onehot[r], preferred_element_type=F32) + jnp.dot(small, onehot[r], preferred_element_type=F32)
            for r in range(2)
        ]
        for d in range(dirs):
            band = slice(d * width, (d + 1) * width)
            pr, pi = gains[0][band, :lanes], gains[1][band, :lanes]
            qr, qi = gains[0][band, lanes:], gains[1][band, lanes:]
            pair_r[d] = pr * qr + pi * qi
            pair_i[d] = pi * qr - pr * qi
        model_r = [jnp.zeros((width, lanes), F32) for _ in range(epochs)]
        model_i = [jnp.zeros((width, lanes), F32) for _ in range(epochs)]
        for s in range(sources):
            which = cluster[s]
            gr, gi = pair_r[which], pair_i[which]
            for t in range(epochs):
                c, n = wave_c[s, t], wave_s[s, t]
                model_r[t] = model_r[t] + (gr * c + gi * n)
                model_i[t] = model_i[t] + (gi * c - gr * n)
        window = taper[chan]
        tiles = []
        for r in range(2):
            for t in range(epochs):
                left = vis_placed[r][t] - (model_r[t] if r == 0 else model_i[t])
                left = (keep[t : t + 1, :] * left).astype(BF16).astype(F32)
                tiles.append((left * window[:, 0:1]).astype(BF16).astype(F32))
        slot = iota((width, 128), 1) // pad
        for c in range(groups):
            tile, place_in = c // per_tile, c % per_tile
            for start in range(0, len(tiles), per_tile):
                block = None
                for j in range(per_tile):
                    piece = tiles[start + j][:, tile * 128 : (tile + 1) * 128]
                    shift = ((j - place_in) * pad) % 128
                    piece = pltpu.roll(piece, shift, 1) if shift else piece
                    block = piece if block is None else jnp.where(slot == j, piece, block)
                out_send[c, :, start * pad : start * pad + 128] = block.astype(BF16)
        out_recv[me] = out_send[chan]

        def push(c, m):
            return pltpu.make_async_remote_copy(
                src_ref=out_send.at[c],
                dst_ref=out_recv.at[me],
                send_sem=a_send,
                recv_sem=a_recv,
                device_id={"chan": c, "tm": m},
                device_id_type=MESH,
            )

        others(lambda c, m: push(c, m).start())

        for r in range(2):
            dual_out[r] = dual[r] + rate * (local[r] - smooth[:, r * half : r * half + stations])
        for copy in first + second:
            copy.wait_send()

        whole = pltpu.make_async_remote_copy(
            src_ref=out_recv.at[pl.ds(0, count - 1)],
            dst_ref=out_recv.at[pl.ds(0, count - 1)],
            send_sem=a_send,
            recv_sem=a_recv,
            device_id={"chan": lax.rem(chan + 1, groups), "tm": part},
            device_id_type=MESH,
        )
        whole.wait_recv()
        wide = total // parts
        kernel_table = table[part]
        cross = jnp.zeros((pad, wide), F32)
        for m in range(parts):
            grid = out_recv[m * groups : (m + 1) * groups].astype(F32).reshape(total, slab)
            raw = jnp.dot(grid.T.astype(BF16), kernel_table, preferred_element_type=F32)
            rest = epochs * pad
            real = raw[:rest, :wide] + raw[rest:, wide:]
            imag = raw[rest:, :wide] - raw[:rest, wide:]
            for j in range(epochs // 2):
                a, b = slice(2 * j * pad, (2 * j + 1) * pad), slice((2 * j + 1) * pad, (2 * j + 2) * pad)
                cross = cross + (real[a] * real[b] + imag[a] * imag[b])
        cross_out[...] = cross[:own] * (norm2 / pair_total)
        whole.wait_send()

    return kernel


def shards(
    visibilities, baseline_coords, source_offsets, source_flux, cluster_of_source,
    baseline_stations, station_flags, local_gains, dual_gains, penalty,
):
    groups, parts = lax.axis_size("chan"), lax.axis_size("tm")
    sources, width = source_flux.shape
    _, epochs, _, base = visibilities.shape
    _, _, _, dirs, stations = local_gains.shape
    total = width * groups
    own = base // groups
    pad = ceil_to(own, 32)
    lanes = groups * pad
    half = ceil_to(stations, 64)
    rows = ceil_to(TERMS * dirs, 8)
    low, high = split_groups(groups)
    tall = dirs * width
    slab = 2 * epochs * pad
    count = groups * parts
    cfg = dict(
        groups=groups, parts=parts, width=width, dirs=dirs, stations=stations, sources=sources, epochs=epochs,
        base=base, own=own, pad=pad, low=low, high=high, rows=rows, total=total, half=half,
    )
    taper = jnp.asarray(np.broadcast_to(taper_values(total).reshape(groups, width, 1), (groups, width, 128)), F32)
    table = delay_tables(total, parts)
    turned = lambda a: a[:, 0].transpose(0, 2, 1, 3).reshape(2, tall, stations)
    vmem = pl.BlockSpec(memory_space=pltpu.VMEM)
    cross, dual = pl.pallas_call(
        make_kernel(cfg),
        out_shape=(
            jax.ShapeDtypeStruct((own, total // parts), F32),
            jax.ShapeDtypeStruct((2, tall, stations), F32),
        ),
        in_specs=[pl.BlockSpec(memory_space=pltpu.SMEM)] + [vmem] * 11,
        out_specs=(vmem, vmem),
        scratch_shapes=[
            pltpu.VMEM((tall, 2 * half), F32),
            pltpu.VMEM((rows, 2 * half), F32),
            pltpu.VMEM((max(low - 1, 1), rows, 2 * half), F32),
            pltpu.VMEM((rows, 2 * half), F32),
            pltpu.VMEM((max(high - 1, 1), rows, 2 * half), F32),
            pltpu.VMEM((base, lanes), BF16),
            pltpu.VMEM((2, 2 * half, 2 * lanes), BF16),
            pltpu.VMEM((epochs, sources, lanes), F32),
            pltpu.VMEM((sources, epochs, width, lanes), F32),
            pltpu.VMEM((sources, epochs, width, lanes), F32),
            pltpu.VMEM((dirs, width, lanes), F32),
            pltpu.VMEM((dirs, width, lanes), F32),
            pltpu.VMEM((groups, width, slab), BF16),
            pltpu.VMEM((count, width, slab), BF16),
            pltpu.SemaphoreType.DMA((max(low - 1, 1),)),
            pltpu.SemaphoreType.DMA((max(low - 1, 1),)),
            pltpu.SemaphoreType.DMA((max(high - 1, 1),)),
            pltpu.SemaphoreType.DMA((max(high - 1, 1),)),
            pltpu.SemaphoreType.DMA,
            pltpu.SemaphoreType.DMA,
        ],
        compiler_params=pltpu.CompilerParams(
            collective_id=0, has_side_effects=True, vmem_limit_bytes=60 * 1024 * 1024
        ),
    )(
        cluster_of_source.reshape(sources), visibilities, baseline_coords, source_offsets, source_flux.T,
        baseline_stations.T, station_flags.T, turned(local_gains), turned(dual_gains), penalty.reshape(1, dirs),
        taper, table,
    )
    dual = dual.reshape(2, dirs, width, stations).transpose(0, 2, 1, 3)[:, None]
    return (cross, dual)


def solution(mesh):
    in_specs = (
        P(None, "tm", "chan", None),
        P(None, "tm", None),
        P(),
        P(None, "chan"),
        P(),
        P(),
        P(None, "tm"),
        P(None, "tm", "chan", None, None),
        P(None, "tm", "chan", None, None),
        P(),
    )
    out_specs = (P("chan", "tm"), P(None, "tm", "chan", None, None))
    return jax.shard_map(shards, mesh=mesh, in_specs=in_specs, out_specs=out_specs, check_vma=False)
```

time: 146 us -> 26.7 us (0.18)
  blocking collectives: 79.4 us -> 0 us
  Pallas kernels: 0 us -> 22.9 us
  local copies, waits for them, and re-layouts: 21.6 us -> 2.9 us
  between operations: 15.3 us -> 0.64 us
  other arithmetic: 11.4 us -> 0 us
  waiting for transfers between devices: 8.69 us -> 0 us
  matrix products: 5.88 us -> 0 us
  starting transfers between devices: 3.53 us -> 0 us
    psum x1 -> x0, blocking collectives: 79.4 us -> none  [shards(): totals = lax.psum(partial_sums, 'chan')]
    pallas_call x0 -> x1, Pallas kernels: none -> 22.9 us  [shards(): pl.pallas_call(make_kernel(cfg), out_shape=(jax.ShapeDtypeStruct((own, to...]
    gather x4 -> x0, local copies, waits for them, and re-layouts: 11 us -> none  [the longest x1 3.91 us: source_model(): jnp.take(coeffs, first, axis=3)]
    all_to_all x1 -> x0, waiting for transfers between devices: 5.62 us -> none  [shards(): lax.all_to_all(residual, 'chan', split_axis=3, concat_axis=2, tiled=True)]
    dot_general x8 -> x0, matrix products: 5.28 us -> none  [the longest x1 1.31 us: shards(): jnp.einsum('fk,rfdp->krdp', basis_local, target, precision=HIGHEST)]
    select_n x4 -> x0, other arithmetic: 4.38 us -> none  [the longest x1 2.73 us: source_model(): jnp.take(coeffs, first, axis=3)]
    all_to_all x1 -> x0, starting transfers between devices: 3.48 us -> none  [shards(): lax.all_to_all(residual, 'chan', split_axis=3, concat_axis=2, tiled=True)]
    reduce_sum x6 -> x0, other arithmetic: 3.48 us -> none  [the longest x5 2.82 us: accumulate(): jnp.sum(part_imag[:, None] * cosine - part_real[:, None] * sine_part, axi...]
  transfers between devices with their start and end apart: 2 -> 0, of which waited for: 2 -> 0; matrix products, arithmetic and copies ran while one was open for 1% -> 0% of each run, Pallas kernels for 0% -> 0%
where the time goes in v1:
time: 26.7 us; the launch traced here: 26.5 us
  Pallas kernels  22.9 us (86%)
  local copies, waits for them, and re-layouts  2.9 us (11%)
  between operations  0.64 us (2%)
    pallas_call x1, Pallas kernels, shards(): pl.pallas_call(make_kernel(cfg), out_shape=(jax.ShapeDtypeStruct((own, to...  22.9 us
    unnamed x2, local copies, waits for them, and re-layouts  2.9 us

profile of v1, /device:TPU:0, one launch (start us, length us, event | category | flops | bytes accessed | tf_op | source)
XLA Modules:
  0.0 26.5 jit_solution(932680193144448230)
XLA Ops:
  0.6 22.9 %shard_map.131 = (f32[30,64]{1,0:T(8,128)}, f32[2,144,62]{2,1,0:T(8,128)}) custom-call(s32[20]{0:T(128)} %bitcast.26, bf16[2,2,8,480]{3,2,1,0:T(8,128)(2,1)} %vis.1, f32[3,2,480]{2,1,0:T(2,128)} %coords.1, f32[2,20]{1,0:T(2,128)} %offsets.1, f32[8,20]{1,0:T(8,128)} %bitcast.23, s32[2,480]{1,0:T(2,128)} %bitcast.24, s32[2,62]{1,0:T(2,128)} %bitcast.25, ...), custom_call_target="tpu_custom_call" | custom-call | tf_op jit(solution)/shard_map/pallas_call | solution.py:335
  23.6 1.3 %copy.16 = f32[30,64]{1,0:T(8,128)} copy(f32[30,64]{1,0:T(8,128)} %get-tuple-element.8) | data formatting | bytes 15360
  24.9 1.6 %copy.17 = f32[2,1,8,18,62]{4,2,3,1,0:T(8,128)} copy(f32[2,1,8,18,62]{4,2,3,1,0:T(8,128)} %bitcast.20) | data formatting | bytes 142848

commit v2 on v1

--- a/solution.py
+++ b/solution.py
@@ -83,8 +83,10 @@
     per_tile = 128 // pad
 
     def kernel(
-        cluster, vis, coords, offsets, flux, pairs, flags, local, dual, penalty, taper, table,
+        cluster_hbm, vis_hbm, coords_hbm, offsets_hbm, flux_hbm, pairs_hbm, flags_hbm, local_hbm, dual_hbm,
+        penalty_hbm, taper_hbm, table_hbm,
         cross_out, dual_out,
+        cluster, vis, coords, offsets, flux, pairs, flags, local, dual, penalty, window_buf, table_buf, load_sem,
         packed, sum_send, sum_recv, part_send, part_recv, perm, onehot, delay, wave_c, wave_s,
         pair_r, pair_i, out_send, out_recv,
         s1_send, s1_recv, s2_send, s2_recv, a_send, a_recv,
@@ -105,16 +107,32 @@
                 first = 1 if dm == 0 else 0
                 lax.fori_loop(first, groups, step, 0, unroll=groups <= 16)
 
-        others(lambda c, m: pl.semaphore_signal(barrier, inc=1, device_id={"chan": c, "tm": m}, device_id_type=MESH))
+        lo, hi = lax.rem(chan, low), chan // low
+
+        def greet(c, m):
+            pl.semaphore_signal(barrier, inc=1, device_id={"chan": c, "tm": m}, device_id_type=MESH)
+
+        for i in range(1, high):
+            greet(lax.rem(hi + i, high) * low + lo, part)
+        for i in range(1, low):
+            greet(hi * low + lax.rem(lo + i, low), part)
+        for i in range(1, parts):
+            greet(chan, lax.rem(part + i, parts))
+        loads = [
+            pltpu.make_async_copy(src, dst, load_sem.at[i])
+            for i, (src, dst) in enumerate(
+                [
+                    (penalty_hbm, penalty), (dual_hbm, dual), (local_hbm, local), (pairs_hbm, pairs),
+                    (coords_hbm, coords), (offsets_hbm, offsets), (flux_hbm, flux), (flags_hbm, flags),
+                    (vis_hbm, vis), (taper_hbm.at[chan], window_buf), (table_hbm.at[part], table_buf),
+                    (cluster_hbm, cluster),
+                ]
+            )
+        ]
+        for load in loads:
+            load.start()
 
         tall = dirs * width
-        rate = jnp.sum(
-            jnp.where(iota((tall, dirs), 0) // width == iota((tall, dirs), 1), penalty[...], 0.0), axis=1, keepdims=True
-        )
-        packed[...] = jnp.zeros_like(packed)
-        inverse_rate = 1.0 / rate
-        for r in range(2):
-            packed[:, r * half : r * half + stations] = local[r] + dual[r] * inverse_rate
 
         def coordinate(f):
             return (2 * (chan * width + f) + 1).astype(F32) / total - 1.0
@@ -128,10 +146,22 @@
         x = coordinate(lax.rem(col, width))
         value = jnp.where(k == 0, 1.0, jnp.where(k == 1, x, 1.5 * x * x - 0.5))
         weights = jnp.where((d == col // width) & (k < TERMS), value, 0.0)
-        sum_send[...] = jnp.dot(weights, packed[...], precision=HIGHEST, preferred_element_type=F32)
-
-        lo, hi = lax.rem(chan, low), chan // low
-        pl.semaphore_wait(barrier, count - 1)
+        prow, pcol = iota((base, lanes), 0), iota((base, lanes), 1)
+        inner = lax.rem(pcol, pad)
+        perm[...] = jnp.where((prow == (pcol // pad) * own + inner) & (inner < own), 1.0, 0.0).astype(BF16)
+        packed[...] = jnp.zeros_like(packed)
+        for load in loads[:3]:
+            load.wait()
+        rate = jnp.sum(
+            jnp.where(iota((tall, dirs), 0) // width == iota((tall, dirs), 1), penalty[...], 0.0), axis=1, keepdims=True
+        )
+        inverse_rate = 1.0 / rate
+        for r in range(2):
+            packed[:, r * half : r * half + stations] = local[r] + dual[r] * inverse_rate
+
+        acc = jnp.dot(weights, packed[...], precision=HIGHEST, preferred_element_type=F32)
+        sum_send[...] = acc
+        pl.semaphore_wait(barrier, low + high + parts - 3)
 
         def stage(src, dst, send, recv, size, mine, address):
             copies = []
@@ -151,10 +181,8 @@
             return copies
 
         first = stage(sum_send, sum_recv, s1_send, s1_recv, low, lo, lambda t: hi * low + t)
-
-        prow, pcol = iota((base, lanes), 0), iota((base, lanes), 1)
-        inner = lax.rem(pcol, pad)
-        perm[...] = jnp.where((prow == (pcol // pad) * own + inner) & (inner < own), 1.0, 0.0).astype(BF16)
+        for load in loads[3:]:
+            load.wait()
         place = perm[...]
         station_rows = jnp.dot(pairs[...].astype(F32).astype(BF16), place, preferred_element_type=F32).astype(jnp.int32)
         srow = iota((2 * half, lanes), 0)
@@ -200,7 +228,6 @@
                     wave_s[s, t] = scale * (turns * horner(SIN_TERMS, z))
 
         phases(0, sources // 2)
-        acc = sum_send[...]
         for i, copy in enumerate(first):
             copy.wait_recv()
             acc = acc + sum_recv[i]
@@ -242,7 +269,7 @@
                 c, n = wave_c[s, t], wave_s[s, t]
                 model_r[t] = model_r[t] + (gr * c + gi * n)
                 model_i[t] = model_i[t] + (gi * c - gr * n)
-        window = taper[chan]
+        window = window_buf[...]
         tiles = []
         for r in range(2):
             for t in range(epochs):
@@ -289,7 +316,7 @@
         )
         whole.wait_recv()
         wide = total // parts
-        kernel_table = table[part]
+        kernel_table = table_buf[...]
         cross = jnp.zeros((pad, wide), F32)
         for m in range(parts):
             grid = out_recv[m * groups : (m + 1) * groups].astype(F32).reshape(total, slab)
@@ -338,9 +365,22 @@
             jax.ShapeDtypeStruct((own, total // parts), F32),
             jax.ShapeDtypeStruct((2, tall, stations), F32),
         ),
-        in_specs=[pl.BlockSpec(memory_space=pltpu.SMEM)] + [vmem] * 11,
+        in_specs=[pl.BlockSpec(memory_space=pltpu.HBM)] * 12,
         out_specs=(vmem, vmem),
         scratch_shapes=[
+            pltpu.SMEM((sources,), jnp.int32),
+            pltpu.VMEM(visibilities.shape, BF16),
+            pltpu.VMEM(baseline_coords.shape, F32),
+            pltpu.VMEM(source_offsets.shape, F32),
+            pltpu.VMEM((width, sources), F32),
+            pltpu.VMEM((2, base), jnp.int32),
+            pltpu.VMEM((epochs, stations), jnp.int32),
+            pltpu.VMEM((2, tall, stations), F32),
+            pltpu.VMEM((2, tall, stations), F32),
+            pltpu.VMEM((1, dirs), F32),
+            pltpu.VMEM((width, 128), F32),
+            pltpu.VMEM((total, 2 * (total // parts)), BF16),
+            pltpu.SemaphoreType.DMA((12,)),
             pltpu.VMEM((tall, 2 * half), F32),
             pltpu.VMEM((rows, 2 * half), F32),
             pltpu.VMEM((max(low - 1, 1), rows, 2 * half), F32),

time: 26.7 us -> 23.6 us (0.88)
  Pallas kernels: 22.9 us -> 19.8 us
    pallas_call x1, Pallas kernels: 22.9 us -> 19.8 us  [shards(): pl.pallas_call(make_kernel(cfg), out_shape=(jax.ShapeDtypeStruct((own, to...]
where the time goes in v2:
time: 23.6 us; the launch traced here: 23.4 us
  Pallas kernels  19.8 us (84%)
  local copies, waits for them, and re-layouts  2.9 us (12%)
  between operations  0.64 us (3%)
    pallas_call x1, Pallas kernels, shards(): pl.pallas_call(make_kernel(cfg), out_shape=(jax.ShapeDtypeStruct((own, to...  19.8 us
    unnamed x2, local copies, waits for them, and re-layouts  2.9 us

profile of v2, /device:TPU:0, one launch (start us, length us, event | category | flops | bytes accessed | tf_op | source)
XLA Modules:
  0.0 23.4 jit_solution(4327978256603444)
XLA Ops:
  0.6 19.8 %shard_map.131 = (f32[30,64]{1,0:T(8,128)}, f32[2,144,62]{2,1,0:T(8,128)}) custom-call(s32[20]{0:T(128)} %bitcast.26, bf16[2,2,8,480]{3,2,1,0:T(8,128)(2,1)} %vis_hbm.1, f32[3,2,480]{2,1,0:T(2,128)} %coords_hbm.1, f32[2,20]{1,0:T(2,128)} %offsets_hbm.1, f32[8,20]{1,0:T(8,128)} %bitcast.23, s32[2,480]{1,0:T(2,128)} %bitcast.24, s32[2,62]{1,0:T(2,128)} %bitcast.25, ...), custom_call_target="tpu_custom_call" | custom-call | tf_op jit(solution)/shard_map/pallas_call | solution.py:362
  20.5 1.3 %copy.16 = f32[30,64]{1,0:T(8,128)} copy(f32[30,64]{1,0:T(8,128)} %get-tuple-element.8) | data formatting | bytes 15360
  21.8 1.6 %copy.17 = f32[2,1,8,18,62]{4,2,3,1,0:T(8,128)} copy(f32[2,1,8,18,62]{4,2,3,1,0:T(8,128)} %bitcast.20) | data formatting | bytes 142848

commit v3 on v2

--- a/solution.py
+++ b/solution.py
@@ -331,6 +331,11 @@
         whole.wait_send()
 
     return kernel
+
+
+def hand_over(cross_in, dual_in, cross_out, dual_out):
+    cross_out[...] = cross_in[...]
+    dual_out[...] = dual_in[...]
 
 
 def shards(
@@ -410,6 +415,15 @@
         baseline_stations.T, station_flags.T, turned(local_gains), turned(dual_gains), penalty.reshape(1, dirs),
         taper, table,
     )
+    cross, dual = pl.pallas_call(
+        hand_over,
+        out_shape=(
+            jax.ShapeDtypeStruct(cross.shape, F32),
+            jax.ShapeDtypeStruct(dual.shape, F32),
+        ),
+        in_specs=[vmem, vmem],
+        out_specs=(vmem, vmem),
+    )(cross, dual)
     dual = dual.reshape(2, dirs, width, stations).transpose(0, 2, 1, 3)[:, None]
     return (cross, dual)
 

time: 23.6 us -> 22.3 us (0.945)
  local copies, waits for them, and re-layouts: 2.9 us -> 0 us
  Pallas kernels: 19.8 us -> 21.4 us
    unnamed x2 -> x0, local copies, waits for them, and re-layouts: 2.9 us -> none
    pallas_call x0 -> x1, Pallas kernels: none -> 1.6 us  [shards(): pl.pallas_call(hand_over, out_shape=(jax.ShapeDtypeStruct(cross.shape, F3...]
where the time goes in v3:
time: 22.3 us; the launch traced here: 22.1 us
  Pallas kernels  21.4 us (96%)
  between operations  0.64 us (3%)
    pallas_call x1, Pallas kernels, shards(): pl.pallas_call(make_kernel(cfg), out_shape=(jax.ShapeDtypeStruct((own, to...  19.8 us
    pallas_call x1, Pallas kernels, shards(): pl.pallas_call(hand_over, out_shape=(jax.ShapeDtypeStruct(cross.shape, F3...  1.6 us

profile of v3, /device:TPU:0, one launch (start us, length us, event | category | flops | bytes accessed | tf_op | source)
XLA Modules:
  0.0 22.1 jit_solution(9904502309586860387)
XLA Ops:
  0.6 19.8 %shard_map.131 = (f32[30,64]{1,0:T(8,128)}, f32[2,144,62]{2,1,0:T(8,128)}) custom-call(s32[20]{0:T(128)} %bitcast.25, bf16[2,2,8,480]{3,2,1,0:T(8,128)(2,1)} %vis_hbm.1, f32[3,2,480]{2,1,0:T(2,128)} %coords_hbm.1, f32[2,20]{1,0:T(2,128)} %offsets_hbm.1, f32[8,20]{1,0:T(8,128)} %bitcast.22, s32[2,480]{1,0:T(2,128)} %bitcast.23, s32[2,62]{1,0:T(2,128)} %bitcast.24, ...), custom_call_target="tpu_custom_call" | custom-call | tf_op jit(solution)/shard_map/pallas_call | solution.py:367
  20.5 1.6 %shard_map.132 = (f32[30,64]{1,0:T(8,128)}, f32[2,144,62]{2,1,0:T(8,128)}) custom-call(f32[30,64]{1,0:T(8,128)} %get-tuple-element.6.cross_in, f32[2,144,62]{2,1,0:T(8,128)} %get-tuple-element.7.dual_in), custom_call_target="tpu_custom_call" | custom-call | tf_op jit(solution)/shard_map/pallas_call | solution.py:418

commit v4 on v3

--- a/solution.py
+++ b/solution.py
@@ -408,7 +408,7 @@
             pltpu.SemaphoreType.DMA,
         ],
         compiler_params=pltpu.CompilerParams(
-            collective_id=0, has_side_effects=True, vmem_limit_bytes=60 * 1024 * 1024
+            collective_id=0, has_side_effects=True, vmem_limit_bytes=40 * 1024 * 1024
         ),
     )(
         cluster_of_source.reshape(sources), visibilities, baseline_coords, source_offsets, source_flux.T,

time: 22.3 us -> 31.5 us (1.41)
  local copies, waits for them, and re-layouts: 0 us -> 9.56 us
  Pallas kernels: 21.4 us -> 20.8 us
    unnamed x0 -> x28, local copies, waits for them, and re-layouts: none -> 9.56 us
    pallas_call x1, Pallas kernels: 19.8 us -> 19.2 us  [shards(): pl.pallas_call(make_kernel(cfg), out_shape=(jax.ShapeDtypeStruct((own, to...]
where the time goes in v4:
time: 31.5 us; the launch traced here: 31 us
  Pallas kernels  20.8 us (66%)
  local copies, waits for them, and re-layouts  9.56 us (30%)
  between operations  0.68 us (2%)
    pallas_call x1, Pallas kernels, shards(): pl.pallas_call(make_kernel(cfg), out_shape=(jax.ShapeDtypeStruct((own, to...  19.2 us
    unnamed x28, local copies, waits for them, and re-layouts  9.56 us
    pallas_call x1, Pallas kernels, shards(): pl.pallas_call(hand_over, out_shape=(jax.ShapeDtypeStruct(cross.shape, F3...  1.6 us

profile of v4, /device:TPU:0, one launch (start us, length us, event | category | flops | bytes accessed | tf_op | source)
XLA Modules:
  0.0 31.0 jit_solution(11535807424263729317)
XLA Ops:
  0.6 0.0 copy-start.7
  0.6 0.0 copy-start.10
  0.7 0.7 %copy-done.7 = f32[3,2,480]{2,1,0:T(2,128)S(1)} copy-done((f32[3,2,480]{2,1,0:T(2,128)S(1)}, f32[3,2,480]{2,1,0:T(2,128)}, u32[]{:S(2)}) %copy-start.7) | copy-done | bytes 11544
  1.3 0.0 copy-done.10
  1.3 0.0 copy-start.1
  1.3 0.9 %copy-done.1 = f32[2,1,8,18,62]{4,2,3,1,0:T(8,128)S(1)} copy-done((f32[2,1,8,18,62]{4,2,3,1,0:T(8,128)S(1)}, f32[2,1,8,18,62]{4,2,3,1,0:T(8,128)}, u32[]{:S(2)}) %copy-start.1) | copy-done | bytes 71448
  2.3 0.0 copy-start.2
  2.3 0.9 %copy-done.2 = f32[2,1,8,18,62]{4,2,3,1,0:T(8,128)S(1)} copy-done((f32[2,1,8,18,62]{4,2,3,1,0:T(8,128)S(1)}, f32[2,1,8,18,62]{4,2,3,1,0:T(8,128)}, u32[]{:S(2)}) %copy-start.2) | copy-done | bytes 71448
  3.2 0.0 copy-start.3
  3.2 0.8 %copy-done.3 = bf16[2,128,128]{2,1,0:T(8,128)(2,1)S(1)} copy-done((bf16[2,128,128]{2,1,0:T(8,128)(2,1)S(1)}, bf16[2,128,128]{2,1,0:T(8,128)(2,1)}, u32[]{:S(2)}) %copy-start.3) | copy-done | bytes 65560
  4.0 0.0 copy-start.4
  4.0 0.8 %copy-done.4 = f32[16,8,128]{2,1,0:T(8,128)S(1)} copy-done((f32[16,8,128]{2,1,0:T(8,128)S(1)}, f32[16,8,128]{2,1,0:T(8,128)}, u32[]{:S(2)}) %copy-start.4) | copy-done | bytes 65560
  4.8 0.0 copy-start.5
  4.8 0.8 %copy-done.5 = bf16[2,2,8,480]{3,2,1,0:T(8,128)(2,1)S(1)} copy-done((bf16[2,2,8,480]{3,2,1,0:T(8,128)(2,1)S(1)}, bf16[2,2,8,480]{3,2,1,0:T(8,128)(2,1)}, u32[]{:S(2)}) %copy-start.5) | copy-done | bytes 30744
  5.6 0.7 %copy-done.8 = f32[20,8]{0,1:T(8,128)S(1)} copy-done((f32[20,8]{0,1:T(8,128)S(1)}, f32[20,8]{0,1:T(8,128)}, u32[]{:S(2)}) %copy-start.8) | copy-done | bytes 664
  6.3 0.7 %copy-done.9 = s32[480,2]{0,1:T(2,128)S(1)} copy-done((s32[480,2]{0,1:T(2,128)S(1)}, s32[480,2]{0,1:T(2,128)}, u32[]{:S(2)}) %copy-start.9) | copy-done | bytes 3864
  7.0 0.7 %copy-done.11 = s32[62,2]{0,1:T(2,128)S(1)} copy-done((s32[62,2]{0,1:T(2,128)S(1)}, s32[62,2]{0,1:T(2,128)}, u32[]{:S(2)}) %copy-start.11) | copy-done | bytes 520
  7.7 0.7 %copy-done.12 = s32[20,1]{0,1:T(1,128)S(1)} copy-done((s32[20,1]{0,1:T(1,128)S(1)}, s32[20,1]{0,1:T(1,128)}, u32[]{:S(2)}) %copy-start.12) | copy-done | bytes 104
  8.3 0.7 %copy-done.13 = f32[18]{0:T(128)S(1)} copy-done((f32[18]{0:T(128)S(1)}, f32[18]{0:T(128)}, u32[]{:S(2)}) %copy-start.13) | copy-done | bytes 96
  9.0 19.2 %shard_map.131 = (f32[30,64]{1,0:T(8,128)S(1)}, f32[2,144,62]{2,1,0:T(8,128)S(1)}) custom-call(s32[20]{0:T(128)S(1)} %bitcast.25, bf16[2,2,8,480]{3,2,1,0:T(8,128)(2,1)S(1)} %copy-done.5, f32[3,2,480]{2,1,0:T(2,128)S(1)} %copy-done.7, f32[2,20]{1,0:T(2,128)S(1)} %copy-done.10, f32[8,20]{1,0:T(8,128)S(1)} %bitcast.22, s32[2,480]{1,0:T(2,128)S(1)} %bitcast.23, ...), custom_call_target="tpu_custom_call" | custom-call | tf_op jit(solution)/shard_map/pallas_call | solution.py:367
  28.1 0.0 copy-start
  28.1 0.6 %copy-done = f32[2,144,62]{2,1,0:T(8,128)} copy-done((f32[2,144,62]{2,1,0:T(8,128)}, f32[2,144,62]{2,1,0:T(8,128)S(1)}, u32[]{:S(2)}) %copy-start) | copy-done | bytes 71448
  28.8 0.6 %copy-done.6 = f32[30,64]{1,0:T(8,128)} copy-done((f32[30,64]{1,0:T(8,128)}, f32[30,64]{1,0:T(8,128)S(1)}, u32[]{:S(2)}) %copy-start.6) | copy-done | bytes 7704
  29.4 1.6 %shard_map.132 = (f32[30,64]{1,0:T(8,128)}, f32[2,144,62]{2,1,0:T(8,128)}) custom-call(f32[30,64]{1,0:T(8,128)} %copy-done.6, f32[2,144,62]{2,1,0:T(8,128)} %copy-done), custom_call_target="tpu_custom_call" | custom-call | tf_op jit(solution)/shard_map/pallas_call | solution.py:418
  (6 shorter events, 0.0 us)
Async XLA Ops:
  0.6 0.7 %copy-start.7 = (f32[3,2,480]{2,1,0:T(2,128)S(1)}, f32[3,2,480]{2,1,0:T(2,128)}, u32[]{:S(2)}) copy-start(f32[3,2,480]{2,1,0:T(2,128)} %coords_hbm.1) | copy-start | bytes 34564
  0.6 0.7 %copy-start.10 = (f32[2,20]{1,0:T(2,128)S(1)}, f32[2,20]{1,0:T(2,128)}, u32[]{:S(2)}) copy-start(f32[2,20]{1,0:T(2,128)} %offsets_hbm.1) | copy-start | bytes 484
  1.3 0.9 %copy-start.1 = (f32[2,1,8,18,62]{4,2,3,1,0:T(8,128)S(1)}, f32[2,1,8,18,62]{4,2,3,1,0:T(8,128)}, u32[]{:S(2)}) copy-start(f32[2,1,8,18,62]{4,2,3,1,0:T(8,128)} %param.19) | copy-start | bytes 214276
  2.3 0.9 %copy-start.2 = (f32[2,1,8,18,62]{4,2,3,1,0:T(8,128)S(1)}, f32[2,1,8,18,62]{4,2,3,1,0:T(8,128)}, u32[]{:S(2)}) copy-start(f32[2,1,8,18,62]{4,2,3,1,0:T(8,128)} %param.20) | copy-start | bytes 214276
  3.2 0.8 %copy-start.3 = (bf16[2,128,128]{2,1,0:T(8,128)(2,1)S(1)}, bf16[2,128,128]{2,1,0:T(8,128)(2,1)}, u32[]{:S(2)}) copy-start(bf16[2,128,128]{2,1,0:T(8,128)(2,1)} %constant.5.clone.table_hbm) | copy-start | bytes 196612
  4.0 0.8 %copy-start.4 = (f32[16,8,128]{2,1,0:T(8,128)S(1)}, f32[16,8,128]{2,1,0:T(8,128)}, u32[]{:S(2)}) copy-start(f32[16,8,128]{2,1,0:T(8,128)} %constant.4.clone.taper_hbm) | copy-start | bytes 196612
  4.8 0.8 %copy-start.5 = (bf16[2,2,8,480]{3,2,1,0:T(8,128)(2,1)S(1)}, bf16[2,2,8,480]{3,2,1,0:T(8,128)(2,1)}, u32[]{:S(2)}) copy-start(bf16[2,2,8,480]{3,2,1,0:T(8,128)(2,1)} %vis_hbm.1) | copy-start | bytes 92164
  5.6 0.7 %copy-start.8 = (f32[20,8]{0,1:T(8,128)S(1)}, f32[20,8]{0,1:T(8,128)}, u32[]{:S(2)}) copy-start(f32[20,8]{0,1:T(8,128)} %param.15) | copy-start | bytes 1924
  6.3 0.7 %copy-start.9 = (s32[480,2]{0,1:T(2,128)S(1)}, s32[480,2]{0,1:T(2,128)}, u32[]{:S(2)}) copy-start(s32[480,2]{0,1:T(2,128)} %param.17) | copy-start | bytes 11524
  7.0 0.7 %copy-start.11 = (s32[62,2]{0,1:T(2,128)S(1)}, s32[62,2]{0,1:T(2,128)}, u32[]{:S(2)}) copy-start(s32[62,2]{0,1:T(2,128)} %param.18) | copy-start | bytes 1492
  7.7 0.7 %copy-start.12 = (s32[20,1]{0,1:T(1,128)S(1)}, s32[20,1]{0,1:T(1,128)}, u32[]{:S(2)}) copy-start(s32[20,1]{0,1:T(1,128)} %param.16) | copy-start | bytes 244
  8.3 0.7 %copy-start.13 = (f32[18]{0:T(128)S(1)}, f32[18]{0:T(128)}, u32[]{:S(2)}) copy-start(f32[18]{0:T(128)} %param.21) | copy-start | bytes 220
  28.1 0.7 %copy-start = (f32[2,144,62]{2,1,0:T(8,128)}, f32[2,144,62]{2,1,0:T(8,128)S(1)}, u32[]{:S(2)}) copy-start(f32[2,144,62]{2,1,0:T(8,128)S(1)} %get-tuple-element.7.dual_in) | copy-start | bytes 214276
  28.8 0.6 %copy-start.6 = (f32[30,64]{1,0:T(8,128)}, f32[30,64]{1,0:T(8,128)S(1)}, u32[]{:S(2)}) copy-start(f32[30,64]{1,0:T(8,128)S(1)} %get-tuple-element.6.cross_in) | copy-start | bytes 23044
